TPU v7x, 512 devices: a whole 4x8x8 slice. The times are simulated.
512 devices in a mesh: gx: 16 (over x, z_lo), gy: 16 (over y, core), af: 2 (over z_hi).
Axes of the slice: x: 4, y: 8, z: 8 (z_hi: 2, z_lo: 4; z = z_hi * 4 + z_lo), core: 2. Of those that a mesh axis runs over, the one named last changes fastest.
Arguments:
- points: bfloat16 [16384, 256], P(('gx', 'gy'), 'af'), may hold values from -12 to 12
- targets: float32 [16384, 16], P(('gx', 'gy')), may hold values from -6 to 6
Outputs:
- solution: float32 [16384, 16], P(('gx', 'gy'))
- residual: float32 [16384, 16], P(('gx', 'gy'))
All inputs are finite; a program needn't handle non-finite values.
Results may differ from a plain program's by a relative error of at most 0.025.
Values may be sent and summed in bfloat16 or wider, within the bound.
A program may use at most 64 MiB of HBM per device.

v0:
```python
import jax
import jax.numpy as jnp
from jax import lax
from jax.sharding import Mesh
from jax.sharding import PartitionSpec as P

ITERS = 2
GY = ("gy_0", "gy_1")
GX = ("gx_0", "gx_1")
GX_GY = ("gx_0", "gx_1", "gy_0", "gy_1")


def laid_out(tiles, dim):
    tiles = jnp.moveaxis(tiles, 0, dim)
    shape = tiles.shape
    return tiles.reshape(*shape[:dim], shape[dim] * shape[dim + 1], *shape[dim + 2 :])


def from_everyone(x, axis):
    copies = jnp.broadcast_to(x, (lax.axis_size(axis), *x.shape))
    return lax.all_to_all(copies, axis, split_axis=0, concat_axis=0, tiled=True)


def gathered_copies(x, axis, dim):
    return laid_out(from_everyone(x, axis), dim)


def split_up(x, dim, count):
    shape = x.shape
    tiles = x.reshape(*shape[:dim], count, shape[dim] // count, *shape[dim + 1 :])
    return jnp.moveaxis(tiles, dim, 0)


def sum_at_owner(x, axis, dim):
    tiles = split_up(x, dim, lax.axis_size(axis))
    arrived = lax.all_to_all(tiles, axis, split_axis=0, concat_axis=0, tiled=True)
    return arrived.astype(jnp.float32).sum(axis=0)


def taken_together(x, axis):
    everything = from_everyone(x, axis)
    return jnp.sum(everything, axis=0)


def by_axis(x, axes):
    far, near = axes
    return taken_together(taken_together(x, near), far)


def in_one(arrays, axis):
    line, at, gathered = (jnp.concatenate([a.reshape(-1) for a in arrays]), 0, [])
    running = by_axis(line, axis)
    for a in arrays:
        gathered.append(running[at : at + a.size].reshape(a.shape))
        at += a.size
    return tuple(gathered)


def point_norms(block):
    wide_block = block.astype(jnp.float32)
    return jnp.sum(wide_block * wide_block, axis=1)


def kernel_times(row_slab, slab_norms, col_slab, col_slab_norms, col_vector, scale):
    inner = lax.dot_general(
        row_slab, col_slab, (((1,), (1,)), ((), ())), preferred_element_type=jnp.float32
    )
    distance = slab_norms[:, None] + col_slab_norms[None, :] - 2.0 * inner
    kernel = jnp.exp(-scale * distance).astype(jnp.bfloat16)
    return jnp.dot(kernel, col_vector, preferred_element_type=jnp.float32)


def split_size(count):
    block_size = count
    while block_size > 1024 and block_size % 2 == 0:
        block_size = block_size // 2
    return block_size


def local(points, targets):
    whole_feat = gathered_copies(points, "af", 1)
    half_rows = whole_feat.shape[0] // 2
    start_row = lax.axis_index("af") * half_rows
    my_points = lax.dynamic_slice_in_dim(whole_feat, start_row, half_rows, 0)
    scale = 0.5 / whole_feat.shape[1]
    row_points = gathered_copies(whole_feat, GY, 0)
    row_norms = point_norms(row_points)
    col_points = gathered_copies(my_points, GX, 0)
    col_norms = point_norms(col_points)

    def operate(vector):
        lowered = vector.astype(jnp.bfloat16)
        my_vector = lax.dynamic_slice_in_dim(lowered, start_row, half_rows, 0)
        col_vector = gathered_copies(my_vector, GX, 0)
        count = vector.shape[0] * lax.axis_size(GY)
        block_size = split_size(count)
        blocks = count // block_size
        row_slab = row_points.reshape(blocks, block_size, row_points.shape[1])
        slab_norms = row_norms.reshape(blocks, block_size)

        def one_block(pair):
            return kernel_times(pair[0], pair[1], col_points, col_norms, col_vector, scale)

        total = sum_at_owner(
            lax.map(one_block, (row_slab, slab_norms))
            .reshape(count, col_vector.shape[1])
            .astype(jnp.bfloat16),
            GY,
            0,
        )
        return taken_together(total, "af") + 0.1 * vector

    def two_products(values, image):
        return in_one(
            (jnp.sum(values * values, axis=0), jnp.sum(values * image, axis=0)),
            (("gx_0", "gx_1"), ("gy_0", "gy_1")),
        )

    solution = jnp.zeros_like(targets)
    residual = targets
    image = operate(residual)
    norm_now, product = two_products(residual, image)
    alpha = norm_now / product
    direction = residual
    along = image
    for step in range(ITERS):
        solution = solution + alpha * direction
        residual = residual - alpha * along
        if step + 1 < ITERS:
            image = operate(residual)
            norm_next, product = two_products(residual, image)
            ratio = norm_next / norm_now
            alpha = norm_next / (product - ratio * norm_next / alpha)
            direction = residual + ratio * direction
            along = image + ratio * along
            norm_now = norm_next
    return (solution, residual)


def solution(mesh):
    torus = Mesh(
        mesh.devices.reshape(4, 4, 8, 2, mesh.shape["af"]), ("gx_0", "gx_1", "gy_0", "gy_1", "af")
    )
    in_specs = (P(GX_GY, "af"), P(GX_GY, None))
    out_specs = (P(GX_GY, None), P(GX_GY, None))
    return jax.shard_map(local, mesh=torus, in_specs=in_specs, out_specs=out_specs, check_vma=False)
```

profile of v0, /device:TPU:1, one launch (start us, length us, event | category | flops | bytes accessed | tf_op | source)
XLA Modules:
  0.0 172.2 jit_solution(2815469622213422851)
XLA Ops:
  0.6 1.3 broadcast_in_dim.52
  2.0 10.8 %all-to-all-start = ((bf16[2,64,128]{2,1,0:T(8,128)(2,1)}), bf16[2,64,128]{2,1,0:T(8,128)(2,1)S(1)}, u32[]{:S(2)}, u32[]{:S(2)}) async-start(bf16[2,64,128]{2,1,0:T(8,128)(2,1)} %broadcast_in_dim.52), calls=%async_computation | async-start | bytes 65536 | tf_op jit(solution)/shard_map/all_to_all | solution.py:21
  12.8 0.8 dynamic-slice_convert_fusion.1
  13.5 0.7 reshape.66
  14.3 5.4 %all-to-all-done = bf16[2,64,128]{2,1,0:T(8,128)(2,1)S(1)} async-done(((bf16[2,64,128]{2,1,0:T(8,128)(2,1)}), bf16[2,64,128]{2,1,0:T(8,128)(2,1)S(1)}, u32[]{:S(2)}, u32[]{:S(2)}) %all-to-all-start) | async-done | bytes 32800 | tf_op jit(solution)/shard_map/all_to_all | solution.py:21
  19.6 6.7 %all-to-all-start.3 = ((bf16[16,2,256]{2,1,0:T(2,128)(2,1)}), bf16[16,2,256]{2,1,0:T(2,128)(2,1)S(1)}, u32[]{:S(2)}, u32[]{:S(2)}) async-start(bf16[16,2,256]{2,1,0:T(2,128)(2,1)} %reshape.66), calls=%async_computation.3 | async-start | bytes 32768 | tf_op jit(solution)/shard_map/all_to_all | solution.py:21
  26.4 6.8 %all-to-all-done.3 = bf16[16,2,256]{2,1,0:T(2,128)(2,1)S(1)} async-done(((bf16[16,2,256]{2,1,0:T(2,128)(2,1)}), bf16[16,2,256]{2,1,0:T(2,128)(2,1)S(1)}, u32[]{:S(2)}, u32[]{:S(2)}) %all-to-all-start.3) | async-done | bytes 16416 | tf_op jit(solution)/shard_map/all_to_all | solution.py:21
  33.1 10.6 %all_to_all.69 = bf16[16,32,256]{2,1,0:T(8,128)(2,1)S(1)} all-to-all(bf16[16,32,256]{2,1,0:T(8,128)(2,1)S(1)} %broadcast_in_dim.54), channel_id=1, replica_groups=mesh['gx_0'=4,'gx_1'=4,'gy_0'=8,'gy_1'=2,'af'=2] {'gx_0','gx_1'}, dimensions={0} | all-to-all | bytes 524288 | tf_op jit(solution)/shard_map/all_to_all | solution.py:21
  43.8 0.8 broadcast_in_dim.53
  44.6 11.8 %all-to-all-start.1 = ((bf16[16,64,256]{2,1,0:T(8,128)(2,1)}), bf16[16,64,256]{2,1,0:T(8,128)(2,1)S(1)}, u32[]{:S(2)}, u32[]{:S(2)}) async-start(bf16[16,64,256]{2,1,0:T(8,128)(2,1)} %broadcast_in_dim.53), calls=%async_computation.1 | async-start | bytes 1048576 | tf_op jit(solution)/shard_map/all_to_all | solution.py:21
  56.6 0.1 multiply_reduce_fusion.1
  56.8 16.7 %all-to-all-done.1 = bf16[16,64,256]{2,1,0:T(8,128)(2,1)S(1)} async-done(((bf16[16,64,256]{2,1,0:T(8,128)(2,1)}), bf16[16,64,256]{2,1,0:T(8,128)(2,1)S(1)}, u32[]{:S(2)}, u32[]{:S(2)}) %all-to-all-start.1) | async-done | bytes 524320 | tf_op jit(solution)/shard_map/all_to_all | solution.py:21
  73.6 0.2 multiply_reduce_fusion
  73.9 0.6 fusion.2
  74.5 0.5 copy.16
  75.1 0.5 fusion.3
  75.6 0.1 reshape.68
  75.7 10.2 %all_to_all.70 = bf16[16,2,512]{2,1,0:T(2,128)(2,1)S(1)} all-to-all(bf16[16,2,512]{2,1,0:T(2,128)(2,1)S(1)} %reshape.68), channel_id=1, replica_groups=mesh['gx_0'=4,'gx_1'=4,'gy_0'=8,'gy_1'=2,'af'=2] {'gy_0','gy_1'}, dimensions={0} | all-to-all | bytes 65536 | tf_op jit(solution)/shard_map/all_to_all | solution.py:36
  86.1 8.9 %all_to_all.71 = f32[2,1,1024]{2,1,0:T(1,128)S(1)} all-to-all(f32[2,1,1024]{2,1,0:T(1,128)S(1)} %reshape.70), channel_id=1, replica_groups=mesh['gx_0'=4,'gx_1'=4,'gy_0'=8,'gy_1'=2,'af'=2] {'af'}, dimensions={0} | all-to-all | bytes 16384 | tf_op jit(solution)/shard_map/all_to_all | solution.py:21
  95.0 0.5 broadcast.42
  95.5 0.7 reduce.6
  96.5 11.0 %all_to_all.72 = f32[16,1,32]{2,1,0:T(1,128)S(1)} all-to-all(f32[16,1,32]{2,1,0:T(1,128)S(1)} %broadcast_in_dim.57), channel_id=1, replica_groups=mesh['gx_0'=4,'gx_1'=4,'gy_0'=8,'gy_1'=2,'af'=2] {'gy_0','gy_1'}, dimensions={0} | all-to-all | bytes 4096 | tf_op jit(solution)/shard_map/all_to_all | solution.py:21
  107.6 9.7 %all_to_all.73 = f32[16,1,32]{2,1,0:T(1,128)S(1)} all-to-all(f32[16,1,32]{2,1,0:T(1,128)S(1)} %broadcast_in_dim.58), channel_id=1, replica_groups=mesh['gx_0'=4,'gx_1'=4,'gy_0'=8,'gy_1'=2,'af'=2] {'gx_0','gx_1'}, dimensions={0} | all-to-all | bytes 4096 | tf_op jit(solution)/shard_map/all_to_all | solution.py:21
  117.7 9.3 %all_to_all.74 = bf16[16,2,256]{2,1,0:T(2,128)(2,1)S(1)} all-to-all(bf16[16,2,256]{2,1,0:T(2,128)(2,1)S(1)} %reshape.72), channel_id=1, replica_groups=mesh['gx_0'=4,'gx_1'=4,'gy_0'=8,'gy_1'=2,'af'=2] {'gx_0','gx_1'}, dimensions={0} | all-to-all | bytes 32768 | tf_op jit(solution)/shard_map/all_to_all | solution.py:21
  127.2 0.5 fusion.4
  127.7 0.1 reshape.74
  127.9 13.1 %all_to_all.75 = bf16[16,2,512]{2,1,0:T(2,128)(2,1)S(1)} all-to-all(bf16[16,2,512]{2,1,0:T(2,128)(2,1)S(1)} %reshape.74), channel_id=1, replica_groups=mesh['gx_0'=4,'gx_1'=4,'gy_0'=8,'gy_1'=2,'af'=2] {'gy_0','gy_1'}, dimensions={0} | all-to-all | bytes 65536 | tf_op jit(solution)/shard_map/all_to_all | solution.py:36
  141.2 8.9 %all_to_all.76 = f32[2,1,1024]{2,1,0:T(1,128)S(1)} all-to-all(f32[2,1,1024]{2,1,0:T(1,128)S(1)} %reshape.76), channel_id=1, replica_groups=mesh['gx_0'=4,'gx_1'=4,'gy_0'=8,'gy_1'=2,'af'=2] {'af'}, dimensions={0} | all-to-all | bytes 16384 | tf_op jit(solution)/shard_map/all_to_all | solution.py:21
  150.1 0.7 reduce.7
  151.1 11.0 %all_to_all.77 = f32[16,1,32]{2,1,0:T(1,128)S(1)} all-to-all(f32[16,1,32]{2,1,0:T(1,128)S(1)} %broadcast_in_dim.61), channel_id=1, replica_groups=mesh['gx_0'=4,'gx_1'=4,'gy_0'=8,'gy_1'=2,'af'=2] {'gy_0','gy_1'}, dimensions={0} | all-to-all | bytes 4096 | tf_op jit(solution)/shard_map/all_to_all | solution.py:21
  162.1 9.3 %all_to_all.78 = f32[16,1,32]{2,1,0:T(1,128)S(1)} all-to-all(f32[16,1,32]{2,1,0:T(1,128)S(1)} %broadcast_in_dim.62), channel_id=1, replica_groups=mesh['gx_0'=4,'gx_1'=4,'gy_0'=8,'gy_1'=2,'af'=2] {'gx_0','gx_1'}, dimensions={0} | all-to-all | bytes 4096 | tf_op jit(solution)/shard_map/all_to_all | solution.py:21
  171.6 0.7 multiply_subtract_fusion
  (44 shorter events, 2.2 us)
Async XLA Ops:
  2.0 17.7 %all-to-all-start = ((bf16[2,64,128]{2,1,0:T(8,128)(2,1)}), bf16[2,64,128]{2,1,0:T(8,128)(2,1)S(1)}, u32[]{:S(2)}, u32[]{:S(2)}) async-start(bf16[2,64,128]{2,1,0:T(8,128)(2,1)} %broadcast_in_dim.52), calls=%async_computation | async-start | bytes 65536 | tf_op jit(solution)/shard_map/all_to_all | solution.py:21
  19.6 13.5 %all-to-all-start.3 = ((bf16[16,2,256]{2,1,0:T(2,128)(2,1)}), bf16[16,2,256]{2,1,0:T(2,128)(2,1)S(1)}, u32[]{:S(2)}, u32[]{:S(2)}) async-start(bf16[16,2,256]{2,1,0:T(2,128)(2,1)} %reshape.66), calls=%async_computation.3 | async-start | bytes 32768 | tf_op jit(solution)/shard_map/all_to_all | solution.py:21
  44.6 29.0 %all-to-all-start.1 = ((bf16[16,64,256]{2,1,0:T(8,128)(2,1)}), bf16[16,64,256]{2,1,0:T(8,128)(2,1)S(1)}, u32[]{:S(2)}, u32[]{:S(2)}) async-start(bf16[16,64,256]{2,1,0:T(8,128)(2,1)} %broadcast_in_dim.53), calls=%async_computation.1 | async-start | bytes 1048576 | tf_op jit(solution)/shard_map/all_to_all | solution.py:21
  75.1 21.2 %copy-start = (f32[64,16]{0,1:T(8,128)S(1)}, f32[64,16]{0,1:T(8,128)}, u32[]{:S(2)}) copy-start(f32[64,16]{0,1:T(8,128)} %param.3) | copy-start | bytes 12292
where the time goes:
time: 173 us; the launch traced here: 172 us
  blocking collectives  102 us (59%)
  starting transfers between devices  29.3 us (17%)
  waiting for transfers between devices  28.9 us (17%)
  local copies, waits for them, and re-layouts  6.41 us (4%)
  other arithmetic  3.14 us (2%)
    all_to_all x8, blocking collectives, from_everyone(): return lax.all_to_all(copies, axis, split_axis=0, concat_axis=0, tiled=True)  78.8 us
    all_to_all x3, starting transfers between devices, from_everyone(): return lax.all_to_all(copies, axis, split_axis=0, concat_axis=0, tiled=True)  29.3 us
    all_to_all x3, waiting for transfers between devices, from_everyone(): return lax.all_to_all(copies, axis, split_axis=0, concat_axis=0, tiled=True)  28.9 us
    all_to_all x2, blocking collectives, sum_at_owner(): lax.all_to_all(tiles, axis, split_axis=0, concat_axis=0, tiled=True)  23.3 us
  transfers between devices with their start and end apart: 3, of which 3 were waited for; matrix products, arithmetic and copies ran while one was open for 1% of the time, Pallas kernels for 0%

commit v1 on v0

v1 whole, which is shorter than its diff:
```python
import math

import jax
import jax.numpy as jnp
from jax import lax
from jax.experimental import pallas as pl
from jax.experimental.pallas import tpu as pltpu
from jax.sharding import Mesh
from jax.sharding import PartitionSpec as P

AXES = ("gx_0", "gx_1", "gy_0", "gy_1", "af")
GX_GY = ("gx_0", "gx_1", "gy_0", "gy_1")
MESH = pl.DeviceIdType.MESH
X, ZL, Y, C, ZH = 4, 4, 8, 2, 2
Z = ZL * ZH
NXZ, NY = X * Z, Y * C
HALF, F, R = 32, 256, 16
F32, BF16 = jnp.float32, jnp.bfloat16


def swap_blocks(tile):
    rows = lax.broadcasted_iota(jnp.int32, (16, 128), 0) // 4
    lanes = lax.broadcasted_iota(jnp.int32, (16, 128), 1) // 32
    shift = (rows - lanes) & 3
    out = tile
    for d in range(1, 4):
        moved = pltpu.roll(pltpu.roll(tile, 128 - 32 * d, 1), 4 * d, 0)
        out = jnp.where(shift == d, moved, out)
    return out


def group_sums(packed):
    group = lax.broadcasted_iota(jnp.int32, (4, 128), 1) // 32
    spread = jnp.concatenate([jnp.where(group == g, packed, 0.0) for g in range(4)], axis=0)
    sums = jnp.sum(spread, axis=1, keepdims=True)
    out = jnp.broadcast_to(sums[12:16], (4, 128))
    for g in range(3):
        out = jnp.where(group == g, sums[4 * g : 4 * g + 4], out)
    return out


def low_lanes():
    return (lax.broadcasted_iota(jnp.int32, (4, 128), 1) & 31) < 16


def paired(first, second):
    return jnp.where(low_lanes(), first, second)


def unpaired(both):
    low = low_lanes()
    return (
        jnp.where(low, both, pltpu.roll(both, 16, 1)),
        jnp.where(low, pltpu.roll(both, 112, 1), both),
    )


def tree_sum(terms):
    while len(terms) > 1:
        terms = [sum(terms[i : i + 2][1:], terms[i]) for i in range(0, len(terms), 2)]
    return terms[0]


def kernel(
    points, targets, solution_ref, residual_ref,
    cols, rows, kmat, vb, vw, vu, bi, wi, ys1, yr1, ys2, yr2, square, send, recv,
):
    x, zl, y, c, zh = (lax.axis_index(a) for a in AXES)
    z = zh * ZL + zl
    me = (x * ZL + zl) * ZH + zh
    mine = y * C + c
    own = (x * ZL + zl) * ZH

    def z_peers():
        for d in (4, 3, 5, 2, 6, 1, 7):
            other = (z + d) % Z
            yield (x, other % ZL, y, c, other // ZL)

    def x_peers():
        for d in (2, 1, 3):
            yield ((x + d) % X, zl, y, c, zh)

    def xz_peers():
        for dz in (4, 3, 5, 2, 6, 1, 7, 0):
            for dx in (2, 1, 3, 0):
                if dz or dx:
                    other = (z + dz) % Z
                    yield ((x + dx) % X, other % ZL, y, c, other // ZL)

    def y_peers():
        for d in (4, 3, 5, 2, 6, 1, 7, 0):
            for e in (1, 0):
                if d or e:
                    yield (x, zl, (y + d) % Y, (c + e) % C, zh)

    def push(src, dst, stage, device):
        pltpu.make_async_remote_copy(
            src_ref=src, dst_ref=dst, send_sem=send.at[stage], recv_sem=recv.at[stage],
            device_id=device, device_id_type=MESH,
        ).start()

    def arrived(ref, stage):
        pltpu.make_async_copy(ref, ref, recv.at[stage]).wait()

    def sent(ref, stage):
        pltpu.make_async_copy(ref, ref, send.at[stage]).wait()

    barrier = pltpu.get_barrier_semaphore()
    greeted = 0
    for peers in (z_peers, x_peers, y_peers):
        for device in peers():
            pl.semaphore_signal(barrier, inc=1, device_id=device, device_id_type=MESH)
            greeted += 1

    square[...] = jnp.zeros_like(square)
    square[0:64, 0:R] = targets[...]
    halves = swap_blocks(jnp.transpose(square[...])[0:16])
    b_own = jnp.where(zh == 0, halves[0:4], halves[4:8])
    vb[me] = jnp.concatenate([b_own, b_own], axis=0)
    bi[mine] = jnp.concatenate([b_own, b_own], axis=0)
    cols[zh, x, zl] = points[...]
    pl.semaphore_wait(barrier, greeted)

    for device in z_peers():
        push(points, cols.at[zh, x, zl], 0, device)
        push(vb.at[me], vb.at[me], 1, device)
    for device in y_peers():
        push(vb.at[me], bi.at[mine], 2, device)
    arrived(rows.at[:, 0:7], 0)
    arrived(vb.at[0:7], 1)

    for device in x_peers():
        push(cols.at[:, x], cols.at[:, x], 3, device)
        push(vb.at[pl.ds(x * Z, Z)], vb.at[pl.ds(x * Z, Z)], 4, device)
    for device in y_peers():
        push(cols.at[:, x, zl, zh], rows.at[:, mine], 5, device)
    rows[:, mine] = cols[:, x, zl, zh]
    arrived(rows.at[:, 0:15], 5)

    scale = 0.5 / F * math.log2(math.e)
    row_points = jnp.concatenate(
        [rows[0].reshape(NY * HALF, 128), rows[1].reshape(NY * HALF, 128)], axis=1
    )
    wide = row_points.astype(F32)
    squares = wide * wide
    high = squares.astype(BF16)
    low = (squares - high.astype(F32)).astype(BF16)
    ones = jnp.ones((8, F), BF16)
    contract = (((1,), (1,)), ((), ()))
    row_norms = (
        lax.dot_general(ones, high, contract, preferred_element_type=F32)
        + lax.dot_general(ones, low, contract, preferred_element_type=F32)
    )[0:1] * scale

    arrived(cols.at[:, 0:3], 3)
    arrived(vb.at[0:24], 4)
    for part in range(X):
        col_points = jnp.concatenate(
            [cols[0, part].reshape(256, 128), cols[1, part].reshape(256, 128)], axis=1
        )
        wide = col_points.astype(F32)
        col_norms = jnp.sum(wide * wide, axis=1, keepdims=True) * scale
        inner = lax.dot_general(col_points, row_points, contract, preferred_element_type=F32)
        kmat[pl.ds(part * 256, 256)] = jnp.exp2(
            (2.0 * scale) * inner - (row_norms + col_norms)
        ).astype(BF16)

    def partial_product(slots):
        wide = [
            swap_blocks(jnp.concatenate(slots[4 * j : 4 * j + 4], axis=0)).astype(BF16)
            for j in range(NXZ // 4)
        ]
        vector = jnp.concatenate(wide, axis=1)
        return jnp.dot(vector, kmat[...], preferred_element_type=F32)

    def to_owners(product, weights, ys, yr, stage):
        blocks = []
        for j in range(NY // 4):
            block = swap_blocks(product[:, 128 * j : 128 * j + 128])
            blocks += [block[4 * s : 4 * s + 4] for s in range(4)]
        share = group_sums(tree_sum([w * b for w, b in zip(weights, blocks)]))
        for t in range(NY):
            ys[t] = jnp.concatenate([blocks[t], share], axis=0)
        for device in y_peers():
            push(ys.at[device[2] * C + device[3]], yr.at[mine], stage, device)
        yr[mine] = ys[mine]
        arrived(yr.at[0:15], stage)
        return tree_sum([yr[t] for t in range(NY)])

    arrived(bi.at[0:15], 2)
    b_rows = [bi[t, 0:4] for t in range(NY)]
    b_cols = [vb[s, 0:4] for s in range(NXZ)]
    total = to_owners(partial_product(b_cols), b_rows, ys1, yr1, 6)
    bb_here = group_sums(tree_sum([b * b for b in b_rows]))
    w_own = total[0:4] + 0.1 * b_own
    vw[me] = jnp.concatenate([w_own, paired(total[4:8], bb_here)], axis=0)
    wi[mine] = jnp.concatenate([w_own, w_own], axis=0)
    for device in xz_peers():
        push(vw.at[me], vw.at[me], 7, device)
    for device in y_peers():
        push(vw.at[me], wi.at[mine], 8, device)
    arrived(vw.at[0:31], 7)
    bkb, bb = unpaired(tree_sum([vw[s, 4:8] for s in range(NXZ)]))
    alpha = bb / (bkb + 0.1 * bb)

    r_cols = [b_cols[s] - alpha * vw[s, 0:4] for s in range(NXZ)]
    product = partial_product(r_cols)
    arrived(wi.at[0:15], 8)
    r_rows = [b_rows[t] - alpha * wi[t, 0:4] for t in range(NY)]
    rr_here = group_sums(tree_sum([r * r for r in r_rows]))
    total = to_owners(product, r_rows, ys2, yr2, 9)
    r_own = b_own - alpha * w_own
    u_own = total[0:4] + 0.1 * r_own
    vu[me] = jnp.concatenate([u_own, paired(total[4:8], rr_here)], axis=0)
    for device in xz_peers():
        push(vu.at[me], vu.at[me], 10, device)
    arrived(vu.at[0:31], 10)
    rkr, rr = unpaired(tree_sum([vu[s, 4:8] for s in range(NXZ)]))
    ratio = rr / bb
    alpha_next = rr / (rkr + 0.1 * rr - ratio * rr / alpha)

    def result(halves, out):
        packed = jnp.concatenate([*halves, jnp.zeros((8, 128), F32)], axis=0)
        square[0:16, :] = swap_blocks(packed)
        out[...] = jnp.transpose(square[...])[0:64, 0:R]

    solutions, residuals = [], []
    for h in range(2):
        b, w, u = vb[own + h, 0:4], vw[own + h, 0:4], vu[own + h, 0:4]
        r = b - alpha * w
        solutions.append(alpha * b + alpha_next * (r + ratio * b))
        residuals.append(r - alpha_next * (u + ratio * w))
    result(solutions, solution_ref)
    result(residuals, residual_ref)

    sent(rows.at[:, 0:7], 0)
    sent(vb.at[0:7], 1)
    sent(bi.at[0:15], 2)
    sent(cols.at[:, 0:3], 3)
    sent(vb.at[0:24], 4)
    sent(rows.at[:, 0:15], 5)
    sent(yr1.at[0:15], 6)
    sent(vw.at[0:31], 7)
    sent(wi.at[0:15], 8)
    sent(yr2.at[0:15], 9)
    sent(vu.at[0:31], 10)


def local(points, targets):
    vmem = pl.BlockSpec(memory_space=pltpu.VMEM)
    message = lambda n: pltpu.VMEM((n, 8, 128), F32)
    return pl.pallas_call(
        kernel,
        out_shape=[jax.ShapeDtypeStruct(targets.shape, F32)] * 2,
        in_specs=[vmem, vmem],
        out_specs=[vmem, vmem],
        scratch_shapes=[
            pltpu.VMEM((2, X, ZL, ZH, HALF, 128), BF16),
            pltpu.VMEM((2, NY, HALF, 128), BF16),
            pltpu.VMEM((NXZ * HALF, NY * HALF), BF16),
            message(NXZ), message(NXZ), message(NXZ),
            message(NY), message(NY),
            message(NY), message(NY), message(NY), message(NY),
            pltpu.VMEM((128, 128), F32),
            pltpu.SemaphoreType.DMA((11,)),
            pltpu.SemaphoreType.DMA((11,)),
        ],
        compiler_params=pltpu.CompilerParams(collective_id=0, has_side_effects=True),
    )(points.reshape(2, HALF, 128), targets)


def solution(mesh):
    torus = Mesh(mesh.devices.reshape(X, ZL, Y, C, ZH), AXES)
    in_specs = (P(GX_GY, "af"), P(GX_GY, None))
    out_specs = (P(GX_GY, None), P(GX_GY, None))
    return jax.shard_map(local, mesh=torus, in_specs=in_specs, out_specs=out_specs, check_vma=False)
```

time: 173 us -> 60.2 us (0.35)
  blocking collectives: 102 us -> 0 us
  Pallas kernels: 0 us -> 55.8 us
  starting transfers between devices: 29.3 us -> 0 us
  waiting for transfers between devices: 28.9 us -> 0 us
  other arithmetic: 3.14 us -> 0 us
  local copies, waits for them, and re-layouts: 6.41 us -> 3.49 us
    all_to_all x10 -> x0, blocking collectives: 102 us -> none  [the longest x8 78.8 us: from_everyone(): return lax.all_to_all(copies, axis, split_axis=0, concat_axis=0, tiled=True)]
    pallas_call x0 -> x1, Pallas kernels: none -> 55.8 us  [local(): pl.pallas_call(kernel, out_shape=[jax.ShapeDtypeStruct(targets.shape, F32...]
    all_to_all x3 -> x0, starting transfers between devices: 29.3 us -> none  [from_everyone(): return lax.all_to_all(copies, axis, split_axis=0, concat_axis=0, tiled=True)]
    all_to_all x3 -> x0, waiting for transfers between devices: 28.9 us -> none  [from_everyone(): return lax.all_to_all(copies, axis, split_axis=0, concat_axis=0, tiled=True)]
    broadcast_in_dim x7 -> x0, local copies, waits for them, and re-layouts: 2.22 us -> none  [from_everyone(): copies = jnp.broadcast_to(x, (lax.axis_size(axis), *x.shape))]
    pallas_call x0 -> x2, local copies, waits for them, and re-layouts: none -> 2.1 us  [local(): pl.pallas_call(kernel, out_shape=[jax.ShapeDtypeStruct(targets.shape, F32...]
  transfers between devices with their start and end apart: 3 -> 0, of which waited for: 3 -> 0; matrix products, arithmetic and copies ran while one was open for 1% -> 0% of each run, Pallas kernels for 0% -> 0%
where the time goes in v1:
time: 60.2 us; the launch traced here: 59.9 us
  Pallas kernels  55.8 us (93%)
  local copies, waits for them, and re-layouts  3.49 us (6%)
  between operations  0.65 us (1%)
    pallas_call x1, Pallas kernels, local(): pl.pallas_call(kernel, out_shape=[jax.ShapeDtypeStruct(targets.shape, F32...  55.8 us
    pallas_call x2, local copies, waits for them, and re-layouts, local(): pl.pallas_call(kernel, out_shape=[jax.ShapeDtypeStruct(targets.shape, F32...  2.1 us
    unnamed x3, local copies, waits for them, and re-layouts  1.39 us

profile of v1, /device:TPU:1, one launch (start us, length us, event | category | flops | bytes accessed | tf_op | source)
XLA Modules:
  0.0 59.9 jit_solution(16990006264410876644)
XLA Ops:
  0.6 1.4 %copy.4.targets = f32[64,16]{1,0:T(8,128)} copy(f32[64,16]{0,1:T(8,128)} %param.3) | data formatting | bytes 8192 | tf_op args[1]
  2.0 55.8 %shard_map.41 = (f32[64,16]{1,0:T(8,128)}, f32[64,16]{1,0:T(8,128)}) custom-call(bf16[2,32,128]{2,1,0:T(8,128)(2,1)} %bitcast.1, f32[64,16]{1,0:T(8,128)} %copy.4.targets), custom_call_target="tpu_custom_call" | custom-call | tf_op jit(solution)/shard_map/pallas_call | solution.py:252
  57.8 0.0 copy-start
  57.8 1.4 %copy.5 = f32[64,16]{0,1:T(8,128)} copy(f32[64,16]{1,0:T(8,128)} %get-tuple-element.2) | data formatting | bytes 8192 | tf_op jit(solution)/shard_map/pallas_call | solution.py:252
  59.2 0.0 copy-done
  59.3 0.7 %copy.6 = f32[64,16]{0,1:T(8,128)} copy(f32[64,16]{1,0:T(8,128)S(1)} %copy-done) | data formatting | bytes 8192 | tf_op jit(solution)/shard_map/pallas_call | solution.py:252
Async XLA Ops:
  57.8 1.4 %copy-start = (f32[64,16]{1,0:T(8,128)S(1)}, f32[64,16]{1,0:T(8,128)}, u32[]{:S(2)}) copy-start(f32[64,16]{1,0:T(8,128)} %get-tuple-element.3) | copy-start | bytes 12292

commit v2 on v1

--- a/solution.py
+++ b/solution.py
@@ -63,7 +63,7 @@
 
 def kernel(
     points, targets, solution_ref, residual_ref,
-    cols, rows, kmat, vb, vw, vu, bi, wi, ys1, yr1, ys2, yr2, square, send, recv,
+    cols, rows, kmat, vb, vw, vu, bi, wi, ys1, yr1, ys2, yr2, send, recv,
 ):
     x, zl, y, c, zh = (lax.axis_index(a) for a in AXES)
     z = zh * ZL + zl
@@ -99,8 +99,11 @@
             device_id=device, device_id_type=MESH,
         ).start()
 
+    pending = []
+
     def arrived(ref, stage):
         pltpu.make_async_copy(ref, ref, recv.at[stage]).wait()
+        pending.append((ref, stage))
 
     def sent(ref, stage):
         pltpu.make_async_copy(ref, ref, send.at[stage]).wait()
@@ -112,29 +115,45 @@
             pl.semaphore_signal(barrier, inc=1, device_id=device, device_id_type=MESH)
             greeted += 1
 
-    square[...] = jnp.zeros_like(square)
-    square[0:64, 0:R] = targets[...]
-    halves = swap_blocks(jnp.transpose(square[...])[0:16])
+    halves = swap_blocks(jnp.concatenate([targets[...], targets[...]], axis=1))
     b_own = jnp.where(zh == 0, halves[0:4], halves[4:8])
-    vb[me] = jnp.concatenate([b_own, b_own], axis=0)
-    bi[mine] = jnp.concatenate([b_own, b_own], axis=0)
+    vb[me] = b_own
+    bi[mine] = b_own
     cols[zh, x, zl] = points[...]
     pl.semaphore_wait(barrier, greeted)
 
+    def z_at(d):
+        other = (z + d) % Z
+        return other // ZL, other % ZL
+
+    def along_x(zh_of, zl_of):
+        block = cols.at[zh_of, x, zl_of]
+        for device in x_peers():
+            push(block, block, 3, device)
+
+    for d in (4, 3, 5, 2, 6, 1, 7):
+        zh_of, zl_of = z_at(d)
+        push(points, cols.at[zh, x, zl], 11 + (Z - d), (x, zl_of, y, c, zh_of))
+    for device in x_peers():
+        push(points, cols.at[zh, x, zl], 3, device)
     for device in z_peers():
-        push(points, cols.at[zh, x, zl], 0, device)
         push(vb.at[me], vb.at[me], 1, device)
     for device in y_peers():
+        push(points.at[zh], rows.at[zh, mine], 5, device)
+    for device in y_peers():
         push(vb.at[me], bi.at[mine], 2, device)
-    arrived(rows.at[:, 0:7], 0)
+    rows[zh, mine] = points[zh]
+    for d in (1, 7, 2, 6, 3, 5):
+        arrived(rows.at[:, 0], 11 + d)
+        along_x(*z_at(d))
+    arrived(rows.at[:, 0], 11 + 4)
+    for device in y_peers():
+        push(cols.at[1 - zh, x, zl, zh], rows.at[1 - zh, mine], 5, device)
+    along_x(1 - zh, zl)
+    rows[1 - zh, mine] = cols[1 - zh, x, zl, zh]
     arrived(vb.at[0:7], 1)
-
     for device in x_peers():
-        push(cols.at[:, x], cols.at[:, x], 3, device)
         push(vb.at[pl.ds(x * Z, Z)], vb.at[pl.ds(x * Z, Z)], 4, device)
-    for device in y_peers():
-        push(cols.at[:, x, zl, zh], rows.at[:, mine], 5, device)
-    rows[:, mine] = cols[:, x, zl, zh]
     arrived(rows.at[:, 0:15], 5)
 
     scale = 0.5 / F * math.log2(math.e)
@@ -188,17 +207,17 @@
         return tree_sum([yr[t] for t in range(NY)])
 
     arrived(bi.at[0:15], 2)
-    b_rows = [bi[t, 0:4] for t in range(NY)]
-    b_cols = [vb[s, 0:4] for s in range(NXZ)]
+    b_rows = [bi[t] for t in range(NY)]
+    b_cols = [vb[s] for s in range(NXZ)]
     total = to_owners(partial_product(b_cols), b_rows, ys1, yr1, 6)
     bb_here = group_sums(tree_sum([b * b for b in b_rows]))
     w_own = total[0:4] + 0.1 * b_own
     vw[me] = jnp.concatenate([w_own, paired(total[4:8], bb_here)], axis=0)
-    wi[mine] = jnp.concatenate([w_own, w_own], axis=0)
+    wi[mine] = w_own
     for device in xz_peers():
         push(vw.at[me], vw.at[me], 7, device)
     for device in y_peers():
-        push(vw.at[me], wi.at[mine], 8, device)
+        push(wi.at[mine], wi.at[mine], 8, device)
     arrived(vw.at[0:31], 7)
     bkb, bb = unpaired(tree_sum([vw[s, 4:8] for s in range(NXZ)]))
     alpha = bb / (bkb + 0.1 * bb)
@@ -206,7 +225,7 @@
     r_cols = [b_cols[s] - alpha * vw[s, 0:4] for s in range(NXZ)]
     product = partial_product(r_cols)
     arrived(wi.at[0:15], 8)
-    r_rows = [b_rows[t] - alpha * wi[t, 0:4] for t in range(NY)]
+    r_rows = [b_rows[t] - alpha * wi[t] for t in range(NY)]
     rr_here = group_sums(tree_sum([r * r for r in r_rows]))
     total = to_owners(product, r_rows, ys2, yr2, 9)
     r_own = b_own - alpha * w_own
@@ -221,52 +240,43 @@
 
     def result(halves, out):
         packed = jnp.concatenate([*halves, jnp.zeros((8, 128), F32)], axis=0)
-        square[0:16, :] = swap_blocks(packed)
-        out[...] = jnp.transpose(square[...])[0:64, 0:R]
+        out[...] = swap_blocks(packed)[:, 0:64]
 
     solutions, residuals = [], []
     for h in range(2):
-        b, w, u = vb[own + h, 0:4], vw[own + h, 0:4], vu[own + h, 0:4]
+        b, w, u = vb[own + h], vw[own + h, 0:4], vu[own + h, 0:4]
         r = b - alpha * w
         solutions.append(alpha * b + alpha_next * (r + ratio * b))
         residuals.append(r - alpha_next * (u + ratio * w))
     result(solutions, solution_ref)
     result(residuals, residual_ref)
 
-    sent(rows.at[:, 0:7], 0)
-    sent(vb.at[0:7], 1)
-    sent(bi.at[0:15], 2)
-    sent(cols.at[:, 0:3], 3)
-    sent(vb.at[0:24], 4)
-    sent(rows.at[:, 0:15], 5)
-    sent(yr1.at[0:15], 6)
-    sent(vw.at[0:31], 7)
-    sent(wi.at[0:15], 8)
-    sent(yr2.at[0:15], 9)
-    sent(vu.at[0:31], 10)
+    for ref, stage in pending:
+        sent(ref, stage)
 
 
 def local(points, targets):
     vmem = pl.BlockSpec(memory_space=pltpu.VMEM)
-    message = lambda n: pltpu.VMEM((n, 8, 128), F32)
-    return pl.pallas_call(
+    message = lambda n, rows=8: pltpu.VMEM((n, rows, 128), F32)
+    turned = targets.T
+    results = pl.pallas_call(
         kernel,
-        out_shape=[jax.ShapeDtypeStruct(targets.shape, F32)] * 2,
+        out_shape=[jax.ShapeDtypeStruct(turned.shape, F32)] * 2,
         in_specs=[vmem, vmem],
         out_specs=[vmem, vmem],
         scratch_shapes=[
             pltpu.VMEM((2, X, ZL, ZH, HALF, 128), BF16),
             pltpu.VMEM((2, NY, HALF, 128), BF16),
             pltpu.VMEM((NXZ * HALF, NY * HALF), BF16),
-            message(NXZ), message(NXZ), message(NXZ),
-            message(NY), message(NY),
+            message(NXZ, 4), message(NXZ), message(NXZ),
+            message(NY, 4), message(NY, 4),
             message(NY), message(NY), message(NY), message(NY),
-            pltpu.VMEM((128, 128), F32),
-            pltpu.SemaphoreType.DMA((11,)),
-            pltpu.SemaphoreType.DMA((11,)),
+            pltpu.SemaphoreType.DMA((19,)),
+            pltpu.SemaphoreType.DMA((19,)),
         ],
         compiler_params=pltpu.CompilerParams(collective_id=0, has_side_effects=True),
-    )(points.reshape(2, HALF, 128), targets)
+    )(points.reshape(2, HALF, 128), turned)
+    return tuple(result.T for result in results)
 
 
 def solution(mesh):

time: 60.2 us -> 55.7 us (0.925)
  Pallas kernels: 55.8 us -> 52.9 us
  local copies, waits for them, and re-layouts: 3.49 us -> 1.9 us
    pallas_call x1, Pallas kernels: 55.8 us -> 52.9 us  [local(): pl.pallas_call(kernel, out_shape=[jax.ShapeDtypeStruct(turned.shape, F32)...]
    pallas_call x2 -> x0, local copies, waits for them, and re-layouts: 2.1 us -> none  [local(): pl.pallas_call(kernel, out_shape=[jax.ShapeDtypeStruct(targets.shape, F32...]
    unnamed x3 -> x4, local copies, waits for them, and re-layouts: 1.39 us -> 1.9 us
where the time goes in v2:
time: 55.7 us; the launch traced here: 55.5 us
  Pallas kernels  52.9 us (95%)
  local copies, waits for them, and re-layouts  1.9 us (3%)
  between operations  0.65 us (1%)
    pallas_call x1, Pallas kernels, local(): pl.pallas_call(kernel, out_shape=[jax.ShapeDtypeStruct(turned.shape, F32)...  52.9 us
    unnamed x4, local copies, waits for them, and re-layouts  1.9 us

profile of v2, /device:TPU:1, one launch (start us, length us, event | category | flops | bytes accessed | tf_op | source)
XLA Modules:
  0.0 55.5 jit_solution(14946005739544662688)
XLA Ops:
  0.6 52.9 %shard_map.41 = (f32[16,64]{1,0:T(8,128)}, f32[16,64]{1,0:T(8,128)}) custom-call(bf16[2,32,128]{2,1,0:T(8,128)(2,1)} %bitcast.4, f32[16,64]{1,0:T(8,128)} %bitcast.5), custom_call_target="tpu_custom_call" | custom-call | tf_op jit(solution)/shard_map/pallas_call | solution.py:262
  53.6 0.0 copy-start
  53.6 1.3 %copy.6 = f32[64,16]{0,1:T(8,128)} copy(f32[64,16]{0,1:T(8,128)} %bitcast.7) | data formatting | bytes 8192
  54.9 0.0 copy-done
  54.9 0.6 %copy.7 = f32[64,16]{0,1:T(8,128)} copy(f32[64,16]{0,1:T(8,128)S(1)} %bitcast.6) | data formatting | bytes 8192
Async XLA Ops:
  53.6 1.3 %copy-start = (f32[16,64]{1,0:T(8,128)S(1)}, f32[16,64]{1,0:T(8,128)}, u32[]{:S(2)}) copy-start(f32[16,64]{1,0:T(8,128)} %get-tuple-element.5) | copy-start | bytes 12292

commit v3 on v2

--- a/solution.py
+++ b/solution.py
@@ -62,8 +62,8 @@
 
 
 def kernel(
-    points, targets, solution_ref, residual_ref,
-    cols, rows, kmat, vb, vw, vu, bi, wi, ys1, yr1, ys2, yr2, send, recv,
+    points, targets, results,
+    turned, cols, rows, kmat, vb, vw, vu, sums, bi, wi, ys1, yr1, ys2, yr2, load, send, recv,
 ):
     x, zl, y, c, zh = (lax.axis_index(a) for a in AXES)
     z = zh * ZL + zl
@@ -108,6 +108,10 @@
     def sent(ref, stage):
         pltpu.make_async_copy(ref, ref, send.at[stage]).wait()
 
+    load_points = pltpu.make_async_copy(points, cols.at[zh, x, zl], load.at[0])
+    load_targets = pltpu.make_async_copy(targets, turned, load.at[1])
+    load_points.start()
+    load_targets.start()
     barrier = pltpu.get_barrier_semaphore()
     greeted = 0
     for peers in (z_peers, x_peers, y_peers):
@@ -115,45 +119,79 @@
             pl.semaphore_signal(barrier, inc=1, device_id=device, device_id_type=MESH)
             greeted += 1
 
-    halves = swap_blocks(jnp.concatenate([targets[...], targets[...]], axis=1))
+    def block_of(d, at_x):
+        other = (z + d) % Z
+        return cols.at[other // ZL, at_x, other % ZL]
+
+    def to_z(d, src, dst, stage):
+        other = (z + d) % Z
+        push(src, dst, stage, (x, other % ZL, y, c, other // ZL))
+
+    def to_x(step, block, stage):
+        push(block, block, stage, ((x + step) % X, zl, y, c, zh))
+
+    def relayed(d):
+        return 1 if d % 2 == 0 else 3
+
+    def along_x(d):
+        block = block_of(d, x)
+        to_x(relayed(d), block, 20 + d)
+        to_x(4 - relayed(d), block, 3)
+
+    def relay(d):
+        arrived(rows.at[:, 0], 20 + d)
+        to_x(relayed(d), block_of(d, (x + 4 - relayed(d)) % X), 28)
+
+    own_block = cols.at[zh, x, zl]
+    load_points.wait()
+    pl.semaphore_wait(barrier, greeted)
+    to_z(4, own_block.at[1 - zh], own_block.at[1 - zh], 0)
+    for d in (1, 7):
+        to_z(d, own_block, own_block, 11 + (Z - d))
+    along_x(0)
+    for d in (2, 6, 3, 5):
+        to_z(d, own_block, own_block, 11 + (Z - d))
+    to_z(4, own_block.at[zh], own_block.at[zh], 11 + 4)
+    for device in y_peers():
+        push(own_block.at[zh], rows.at[zh, mine], 5, device)
+    rows[zh, mine] = cols[zh, x, zl, zh]
+
+    load_targets.wait()
+    halves = swap_blocks(jnp.concatenate([turned[...], turned[...]], axis=1))
     b_own = jnp.where(zh == 0, halves[0:4], halves[4:8])
     vb[me] = b_own
     bi[mine] = b_own
-    cols[zh, x, zl] = points[...]
-    pl.semaphore_wait(barrier, greeted)
-
-    def z_at(d):
-        other = (z + d) % Z
-        return other // ZL, other % ZL
-
-    def along_x(zh_of, zl_of):
-        block = cols.at[zh_of, x, zl_of]
-        for device in x_peers():
-            push(block, block, 3, device)
-
-    for d in (4, 3, 5, 2, 6, 1, 7):
-        zh_of, zl_of = z_at(d)
-        push(points, cols.at[zh, x, zl], 11 + (Z - d), (x, zl_of, y, c, zh_of))
-    for device in x_peers():
-        push(points, cols.at[zh, x, zl], 3, device)
     for device in z_peers():
         push(vb.at[me], vb.at[me], 1, device)
     for device in y_peers():
-        push(points.at[zh], rows.at[zh, mine], 5, device)
-    for device in y_peers():
-        push(vb.at[me], bi.at[mine], 2, device)
-    rows[zh, mine] = points[zh]
-    for d in (1, 7, 2, 6, 3, 5):
+        push(bi.at[mine], bi.at[mine], 2, device)
+
+    for d in (1, 7):
         arrived(rows.at[:, 0], 11 + d)
-        along_x(*z_at(d))
-    arrived(rows.at[:, 0], 11 + 4)
+        along_x(d)
+    relay(0)
+    for d in (2, 6):
+        arrived(rows.at[:, 0], 11 + d)
+        along_x(d)
+    arrived(rows.at[0, 0], 0)
     for device in y_peers():
         push(cols.at[1 - zh, x, zl, zh], rows.at[1 - zh, mine], 5, device)
-    along_x(1 - zh, zl)
     rows[1 - zh, mine] = cols[1 - zh, x, zl, zh]
+    relay(1)
+    relay(7)
+    for d in (3, 5):
+        arrived(rows.at[:, 0], 11 + d)
+        along_x(d)
+    relay(2)
+    relay(6)
+    arrived(rows.at[0, 0], 11 + 4)
+    along_x(4)
     arrived(vb.at[0:7], 1)
     for device in x_peers():
         push(vb.at[pl.ds(x * Z, Z)], vb.at[pl.ds(x * Z, Z)], 4, device)
+    relay(3)
+    relay(5)
+    relay(4)
     arrived(rows.at[:, 0:15], 5)
 
     scale = 0.5 / F * math.log2(math.e)
@@ -171,18 +209,22 @@
         + lax.dot_general(ones, low, contract, preferred_element_type=F32)
     )[0:1] * scale
 
-    arrived(cols.at[:, 0:3], 3)
-    arrived(vb.at[0:24], 4)
-    for part in range(X):
+    for d in range(X):
+        if d == 1:
+            arrived(rows.at[:, 0:8], 3)
+            arrived(rows.at[:, 0:8], 28)
+        part = (x + d) % X
         col_points = jnp.concatenate(
             [cols[0, part].reshape(256, 128), cols[1, part].reshape(256, 128)], axis=1
         )
         wide = col_points.astype(F32)
         col_norms = jnp.sum(wide * wide, axis=1, keepdims=True) * scale
         inner = lax.dot_general(col_points, row_points, contract, preferred_element_type=F32)
-        kmat[pl.ds(part * 256, 256)] = jnp.exp2(
+        kmat[part] = jnp.exp2(
             (2.0 * scale) * inner - (row_norms + col_norms)
         ).astype(BF16)
+
+    arrived(vb.at[0:24], 4)
 
     def partial_product(slots):
         wide = [
@@ -190,7 +232,7 @@
             for j in range(NXZ // 4)
         ]
         vector = jnp.concatenate(wide, axis=1)
-        return jnp.dot(vector, kmat[...], preferred_element_type=F32)
+        return jnp.dot(vector, kmat[...].reshape(NXZ * HALF, NY * HALF), preferred_element_type=F32)
 
     def to_owners(product, weights, ys, yr, stage):
         blocks = []
@@ -230,11 +272,13 @@
     total = to_owners(product, r_rows, ys2, yr2, 9)
     r_own = b_own - alpha * w_own
     u_own = total[0:4] + 0.1 * r_own
-    vu[me] = jnp.concatenate([u_own, paired(total[4:8], rr_here)], axis=0)
+    sums[me] = paired(total[4:8], rr_here)
     for device in xz_peers():
-        push(vu.at[me], vu.at[me], 10, device)
-    arrived(vu.at[0:31], 10)
-    rkr, rr = unpaired(tree_sum([vu[s, 4:8] for s in range(NXZ)]))
+        push(sums.at[me], sums.at[me], 10, device)
+    vu[zh] = u_own
+    to_z(4, vu.at[zh], vu.at[zh], 9 + 20)
+    arrived(sums.at[0:31], 10)
+    rkr, rr = unpaired(tree_sum([sums[s] for s in range(NXZ)]))
     ratio = rr / bb
     alpha_next = rr / (rkr + 0.1 * rr - ratio * rr / alpha)
 
@@ -242,41 +286,43 @@
         packed = jnp.concatenate([*halves, jnp.zeros((8, 128), F32)], axis=0)
         out[...] = swap_blocks(packed)[:, 0:64]
 
+    arrived(vu.at[0], 29)
     solutions, residuals = [], []
     for h in range(2):
-        b, w, u = vb[own + h], vw[own + h, 0:4], vu[own + h, 0:4]
+        b, w, u = vb[own + h], vw[own + h, 0:4], vu[h]
         r = b - alpha * w
         solutions.append(alpha * b + alpha_next * (r + ratio * b))
         residuals.append(r - alpha_next * (u + ratio * w))
-    result(solutions, solution_ref)
-    result(residuals, residual_ref)
+    result(solutions, results.at[0])
+    result(residuals, results.at[1])
 
     for ref, stage in pending:
         sent(ref, stage)
 
 
 def local(points, targets):
-    vmem = pl.BlockSpec(memory_space=pltpu.VMEM)
+    anywhere = pl.BlockSpec(memory_space=pl.ANY)
     message = lambda n, rows=8: pltpu.VMEM((n, rows, 128), F32)
-    turned = targets.T
     results = pl.pallas_call(
         kernel,
-        out_shape=[jax.ShapeDtypeStruct(turned.shape, F32)] * 2,
-        in_specs=[vmem, vmem],
-        out_specs=[vmem, vmem],
+        out_shape=pltpu.VMEM((2, R, 2 * HALF), F32),
+        in_specs=[anywhere, anywhere],
+        out_specs=pl.BlockSpec(memory_space=pltpu.VMEM),
         scratch_shapes=[
+            pltpu.VMEM((R, 2 * HALF), F32),
             pltpu.VMEM((2, X, ZL, ZH, HALF, 128), BF16),
             pltpu.VMEM((2, NY, HALF, 128), BF16),
-            pltpu.VMEM((NXZ * HALF, NY * HALF), BF16),
-            message(NXZ, 4), message(NXZ), message(NXZ),
+            pltpu.VMEM((X, Z * HALF, NY * HALF), BF16),
+            message(NXZ, 4), message(NXZ), message(ZH, 4), message(NXZ, 4),
             message(NY, 4), message(NY, 4),
             message(NY), message(NY), message(NY), message(NY),
-            pltpu.SemaphoreType.DMA((19,)),
-            pltpu.SemaphoreType.DMA((19,)),
+            pltpu.SemaphoreType.DMA((2,)),
+            pltpu.SemaphoreType.DMA((30,)),
+            pltpu.SemaphoreType.DMA((30,)),
         ],
         compiler_params=pltpu.CompilerParams(collective_id=0, has_side_effects=True),
-    )(points.reshape(2, HALF, 128), turned)
-    return tuple(result.T for result in results)
+    )(points.reshape(2, HALF, 128), targets.T)
+    return results[0].T, results[1].T
 
 
 def solution(mesh):

time: 55.7 us -> 54.5 us (0.978)
  local copies, waits for them, and re-layouts: 1.9 us -> 0.61 us
    unnamed x4 -> x0, local copies, waits for them, and re-layouts: 1.9 us -> none
    transpose x0 -> x1, local copies, waits for them, and re-layouts: none -> 0.61 us  [local(): return (results[0].T, results[1].T)]
where the time goes in v3:
time: 54.5 us; the launch traced here: 54.3 us
  Pallas kernels  53.1 us (97%)
  between operations  0.64 us (1%)
  local copies, waits for them, and re-layouts  0.61 us (1%)
    pallas_call x1, Pallas kernels, local(): pl.pallas_call(kernel, out_shape=pltpu.VMEM((2, R, 2 * HALF), F32), in_sp...  53.1 us

profile of v3, /device:TPU:1, one launch (start us, length us, event | category | flops | bytes accessed | tf_op | source)
XLA Modules:
  0.0 54.3 jit_solution(6767733882470598558)
XLA Ops:
  0.6 53.1 %shard_map.41 = f32[2,16,64]{2,1,0:T(8,128)S(1)} custom-call(bf16[2,32,128]{2,1,0:T(8,128)(2,1)} %bitcast.10, f32[16,64]{1,0:T(8,128)} %bitcast.11), custom_call_target="tpu_custom_call" | custom-call | tf_op jit(solution)/shard_map/pallas_call | solution.py:306
  53.7 0.6 %slice_bitcast_fusion = (f32[64,16]{0,1:T(8,128)}, f32[64,16]{0,1:T(8,128)}) fusion(f32[2,16,64]{2,1,0:T(8,128)S(1)} %shard_map.41), kind=kLoop, calls=%fused_computation | loop fusion | bytes 16384 | tf_op jit(solution)/shard_map/transpose | solution.py:325

commit v4 on v3

--- a/solution.py
+++ b/solution.py
@@ -130,17 +130,10 @@
     def to_x(step, block, stage):
         push(block, block, stage, ((x + step) % X, zl, y, c, zh))
 
-    def relayed(d):
-        return 1 if d % 2 == 0 else 3
-
     def along_x(d):
         block = block_of(d, x)
-        to_x(relayed(d), block, 20 + d)
-        to_x(4 - relayed(d), block, 3)
-
-    def relay(d):
-        arrived(rows.at[:, 0], 20 + d)
-        to_x(relayed(d), block_of(d, (x + 4 - relayed(d)) % X), 28)
+        for step in (2, 1, 3):
+            to_x(step, block, 3)
 
     own_block = cols.at[zh, x, zl]
     load_points.wait()
@@ -169,7 +162,6 @@
     for d in (1, 7):
         arrived(rows.at[:, 0], 11 + d)
         along_x(d)
-    relay(0)
     for d in (2, 6):
         arrived(rows.at[:, 0], 11 + d)
         along_x(d)
@@ -177,21 +169,14 @@
     for device in y_peers():
         push(cols.at[1 - zh, x, zl, zh], rows.at[1 - zh, mine], 5, device)
     rows[1 - zh, mine] = cols[1 - zh, x, zl, zh]
-    relay(1)
-    relay(7)
     for d in (3, 5):
         arrived(rows.at[:, 0], 11 + d)
         along_x(d)
-    relay(2)
-    relay(6)
     arrived(rows.at[0, 0], 11 + 4)
     along_x(4)
     arrived(vb.at[0:7], 1)
     for device in x_peers():
         push(vb.at[pl.ds(x * Z, Z)], vb.at[pl.ds(x * Z, Z)], 4, device)
-    relay(3)
-    relay(5)
-    relay(4)
     arrived(rows.at[:, 0:15], 5)
 
     scale = 0.5 / F * math.log2(math.e)
@@ -211,8 +196,7 @@
 
     for d in range(X):
         if d == 1:
-            arrived(rows.at[:, 0:8], 3)
-            arrived(rows.at[:, 0:8], 28)
+            arrived(cols.at[:, 0:3], 3)
         part = (x + d) % X
         col_points = jnp.concatenate(
             [cols[0, part].reshape(256, 128), cols[1, part].reshape(256, 128)], axis=1
@@ -276,7 +260,7 @@
     for device in xz_peers():
         push(sums.at[me], sums.at[me], 10, device)
     vu[zh] = u_own
-    to_z(4, vu.at[zh], vu.at[zh], 9 + 20)
+    to_z(4, vu.at[zh], vu.at[zh], 19)
     arrived(sums.at[0:31], 10)
     rkr, rr = unpaired(tree_sum([sums[s] for s in range(NXZ)]))
     ratio = rr / bb
@@ -286,7 +270,7 @@
         packed = jnp.concatenate([*halves, jnp.zeros((8, 128), F32)], axis=0)
         out[...] = swap_blocks(packed)[:, 0:64]
 
-    arrived(vu.at[0], 29)
+    arrived(vu.at[0], 19)
     solutions, residuals = [], []
     for h in range(2):
         b, w, u = vb[own + h], vw[own + h, 0:4], vu[h]
@@ -317,8 +301,8 @@
             message(NY, 4), message(NY, 4),
             message(NY), message(NY), message(NY), message(NY),
             pltpu.SemaphoreType.DMA((2,)),
-            pltpu.SemaphoreType.DMA((30,)),
-            pltpu.SemaphoreType.DMA((30,)),
+            pltpu.SemaphoreType.DMA((20,)),
+            pltpu.SemaphoreType.DMA((20,)),
         ],
         compiler_params=pltpu.CompilerParams(collective_id=0, has_side_effects=True),
     )(points.reshape(2, HALF, 128), targets.T)

time: 54.5 us -> 50.2 us (0.921)
  Pallas kernels: 53.1 us -> 48.8 us
    pallas_call x1, Pallas kernels: 53.1 us -> 48.8 us  [local(): pl.pallas_call(kernel, out_shape=pltpu.VMEM((2, R, 2 * HALF), F32), in_sp...]
where the time goes in v4:
time: 50.2 us; the launch traced here: 50.1 us
  Pallas kernels  48.8 us (97%)
  between operations  0.64 us (1%)
  local copies, waits for them, and re-layouts  0.61 us (1%)
    pallas_call x1, Pallas kernels, local(): pl.pallas_call(kernel, out_shape=pltpu.VMEM((2, R, 2 * HALF), F32), in_sp...  48.8 us

profile of v4, /device:TPU:1, one launch (start us, length us, event | category | flops | bytes accessed | tf_op | source)
XLA Modules:
  0.0 50.1 jit_solution(10888928114615112988)
XLA Ops:
  0.6 48.8 %shard_map.41 = f32[2,16,64]{2,1,0:T(8,128)S(1)} custom-call(bf16[2,32,128]{2,1,0:T(8,128)(2,1)} %bitcast.10, f32[16,64]{1,0:T(8,128)} %bitcast.11), custom_call_target="tpu_custom_call" | custom-call | tf_op jit(solution)/shard_map/pallas_call | solution.py:290
  49.5 0.6 %slice_bitcast_fusion = (f32[64,16]{0,1:T(8,128)}, f32[64,16]{0,1:T(8,128)}) fusion(f32[2,16,64]{2,1,0:T(8,128)S(1)} %shard_map.41), kind=kLoop, calls=%fused_computation | loop fusion | bytes 16384 | tf_op jit(solution)/shard_map/transpose | solution.py:309
